TPU v7x, 32 devices: a whole 2x2x4 slice. The times are simulated.
32 devices in a mesh: section: 4 (over y, x), dp: 8 (over z, core).
Axes of the slice: x: 2, y: 2, z: 4, core: 2. Of those that a mesh axis runs over, the one named last changes fastest.
Arguments:
- block_inputs: bfloat16 [4, 4, 512, 2048], P('section', None, 'dp'), may hold values from -6 to 6
- mixed_inputs: bfloat16 [4, 4, 512, 2048], P('section', None, 'dp'), may hold values from -6 to 6
- token_ids: int32 [4, 512], P(None, 'dp'), may hold values from 0 to 2047
- target_ids: int32 [4, 512], P(None, 'dp'), may hold values from 0 to 2047
- final_gain: float32 [2048], replicated, may hold values from 0.5 to 1.5
- out_weight: bfloat16 [4, 2048, 2048], P('section'), may hold values from -0.0625 to 0.0625
- head_weight: bfloat16 [2048, 2048], P('section'), may hold values from -0.375 to 0.375
- out_master: float32 [4, 2048, 2048], P('section', 'dp'), may hold values from -0.125 to 0.125
- out_first: float32 [4, 2048, 2048], P('section', 'dp'), may hold values from -1.25 to 1.25
- out_second: float32 [4, 2048, 2048], P('section', 'dp'), may hold values from 1 to 20
- head_master: float32 [2048, 2048], P(('section', 'dp')), may hold values from -0.125 to 0.125
- head_first: float32 [2048, 2048], P(('section', 'dp')), may hold values from -0.75 to 0.75
- head_second: float32 [2048, 2048], P(('section', 'dp')), may hold values from 0.3 to 6
- embed_master: float32 [2048, 2048], P(('section', 'dp')), may hold values from -0.125 to 0.125
- embed_first: float32 [2048, 2048], P(('section', 'dp')), may hold values from -0.0625 to 0.0625
- embed_second: float32 [2048, 2048], P(('section', 'dp')), may hold values from 0.0024414062 to 0.048828125
Outputs:
- out_master_next: float32 [4, 2048, 2048], P('section', 'dp')
- out_first_next: float32 [4, 2048, 2048], P('section', 'dp')
- out_second_next: float32 [4, 2048, 2048], P('section', 'dp')
- head_master_next: float32 [2048, 2048], P(('section', 'dp'))
- head_first_next: float32 [2048, 2048], P(('section', 'dp'))
- head_second_next: float32 [2048, 2048], P(('section', 'dp'))
- embed_master_next: float32 [2048, 2048], P(('section', 'dp'))
- embed_first_next: float32 [2048, 2048], P(('section', 'dp'))
- embed_second_next: float32 [2048, 2048], P(('section', 'dp'))
Inputs may be any that keep to these rules, and one draw needn't show every extreme that they name: `token_ids`: every token id lies in 0 to 2047. `target_ids`: every target id lies in 0 to 2047.
All inputs are finite; a program needn't handle non-finite values.
Results may differ from a plain program's by a relative error of at most 0.00155.
Values may be sent and summed in bfloat16 or wider, within the bound.
A program may use at most 128 MiB of HBM per device.

v0:
```python
import jax
import jax.numpy as jnp
from jax import lax
from jax.sharding import PartitionSpec as P

norm_eps = 1e-05
beta_first = 0.9
beta_second = 0.95
adam_eps = 1e-05
learning_rate = 0.0003
decay_rate = 0.1


def broadcast(value, axis, source):
    kept = jnp.where(lax.axis_index(axis) == source, value, 0).astype(value.dtype)
    return lax.psum(kept, axis)


def combined_all(part, axis, combine):
    gathered = jax.tree.map(lambda a: lax.all_gather(a, axis), part)

    def take(source):
        return jax.tree.map(lambda a: lax.dynamic_index_in_dim(a, source, 0, False), gathered)

    return lax.fori_loop(
        1, lax.axis_size(axis), lambda source, state: combine(state, take(source)), take(0)
    )


def from_behind(block, axis, distance):
    devices = range(lax.axis_size(axis))
    route = [(i - distance, i) for i in devices if i - distance in devices]
    return lax.ppermute(block, axis, route)


def times_transposed(former, latter):
    return lax.dot_general(
        former, latter, (((1,), (1,)), ((), ())), preferred_element_type=jnp.float32
    )


def transposed_times(former, latter):
    return lax.dot_general(
        former, latter, (((0,), (0,)), ((), ())), preferred_element_type=jnp.float32
    )


def plain_times(former, latter):
    return jnp.dot(former, latter, preferred_element_type=jnp.float32)


def normalize(values, gain):
    inverse = lax.rsqrt(jnp.mean(values * values, axis=-1, keepdims=True) + norm_eps)
    return (inverse, values * inverse * gain)


def norm_backward(values, inverse, scaled_cotangent):
    unit = values * inverse
    return inverse * (
        scaled_cotangent - unit * jnp.mean(scaled_cotangent * unit, axis=-1, keepdims=True)
    )


def adam_update(master, first, second, gradient):
    first_next = beta_first * first + (1.0 - beta_first) * gradient
    second_next = beta_second * second + (1.0 - beta_second) * gradient * gradient
    master_next = master - learning_rate * (
        first_next / (jnp.sqrt(second_next) + adam_eps) + decay_rate * master
    )
    return (master_next, first_next, second_next)


def join_rows(former, latter):
    top = jnp.maximum(former[0], latter[0])
    return (top, former[1] * jnp.exp(former[0] - top) + latter[1] * jnp.exp(latter[0] - top))


def local(
    block_inputs,
    mixed_inputs,
    token_ids,
    target_ids,
    final_gain,
    out_weight,
    head_weight,
    out_master,
    out_first,
    out_second,
    head_master,
    head_first,
    head_second,
    embed_master,
    embed_first,
    embed_second,
):
    sections = lax.axis_size("section")
    section = lax.axis_index("section")
    last = sections - 1
    batches, rows, width = mixed_inputs[0].shape
    flat_mixed = mixed_inputs[0].reshape(batches * rows, width)
    wide = block_inputs[0].reshape(batches * rows, width).astype(jnp.float32)
    slice_rows = head_weight.shape[0]
    vocabulary_start = section * slice_rows
    columns = vocabulary_start + lax.broadcasted_iota(jnp.int32, (1, slice_rows), 1)
    final = wide + times_transposed(flat_mixed, out_weight[0])
    final_inverse, final_scaled = normalize(final, final_gain)
    shared_hidden = broadcast(final_scaled.astype(jnp.bfloat16), "section", last)
    logits = times_transposed(shared_hidden, head_weight)
    local_top = jnp.max(logits, axis=1)
    local_weights = jnp.exp(logits - local_top[:, None])
    row_top, row_total = combined_all(
        (local_top, jnp.sum(local_weights, axis=1)), "section", join_rows
    )
    predicted = local_weights * (jnp.exp(local_top - row_top) / row_total)[:, None]
    target_flat = target_ids.reshape(-1)
    logit_cotangent = jnp.where(target_flat[:, None] == columns, predicted - 1.0, predicted).astype(
        jnp.bfloat16
    )
    hidden_cotangent = lax.psum(plain_times(logit_cotangent, head_weight), "section")
    top_cotangent = norm_backward(final, final_inverse, hidden_cotangent * final_gain).astype(
        jnp.bfloat16
    )

    def reduce_head():

        def head_term(count):
            part = lax.slice_in_dim(logit_cotangent, 0, count, axis=1)
            return transposed_times(part, shared_hidden)

        return lax.psum_scatter(
            head_term(head_master.shape[0] * lax.axis_size("dp")),
            "dp",
            scatter_dimension=0,
            tiled=True,
        )

    def relay(step, held):
        received = from_behind(held, "section", -1)
        return jnp.where(section == last, held, received)

    cotangent = lax.fori_loop(0, last, relay, top_cotangent)
    out_term = transposed_times(cotangent, flat_mixed)
    out_gradient = lax.psum_scatter(out_term, "dp", scatter_dimension=0, tiled=True)
    tokens_flat = token_ids.reshape(-1)

    def embed_term(count):
        wanted = vocabulary_start + lax.broadcasted_iota(jnp.int32, (1, count), 1)
        marks = (tokens_flat[:, None] == wanted).astype(jnp.bfloat16)
        return transposed_times(marks, cotangent)

    embed_gradient = lax.psum_scatter(
        embed_term(embed_master.shape[0] * lax.axis_size("dp")),
        "dp",
        scatter_dimension=0,
        tiled=True,
    )
    head_gradient = reduce_head()
    out_out = adam_update(out_master, out_first, out_second, out_gradient.reshape(out_master.shape))
    head_out = adam_update(head_master, head_first, head_second, head_gradient)
    embed_out = adam_update(embed_master, embed_first, embed_second, embed_gradient)
    return (
        out_out[0],
        out_out[1],
        out_out[2],
        head_out[0],
        head_out[1],
        head_out[2],
        embed_out[0],
        embed_out[1],
        embed_out[2],
    )


def solution(mesh):
    return jax.shard_map(
        local,
        mesh=mesh,
        in_specs=(
            P("section", None, "dp", None),
            P("section", None, "dp", None),
            P(None, "dp"),
            P(None, "dp"),
            P(),
            P("section", None, None),
            P("section", None),
            P("section", "dp", None),
            P("section", "dp", None),
            P("section", "dp", None),
            P(("section", "dp"), None),
            P(("section", "dp"), None),
            P(("section", "dp"), None),
            P(("section", "dp"), None),
            P(("section", "dp"), None),
            P(("section", "dp"), None),
        ),
        out_specs=(
            P("section", "dp", None),
            P("section", "dp", None),
            P("section", "dp", None),
            P(("section", "dp"), None),
            P(("section", "dp"), None),
            P(("section", "dp"), None),
            P(("section", "dp"), None),
            P(("section", "dp"), None),
            P(("section", "dp"), None),
        ),
        check_vma=False,
    )
```

profile of v0, /device:TPU:0, one launch (start us, length us, event | category | flops | bytes accessed | tf_op | source)
XLA Modules:
  0.0 482.8 jit_solution(1719331455801563350)
XLA Ops:
  7.3 7.8 %multiply_reduce_fusion.1 = (f32[256]{0:T(256)S(1)}, f32[256,2048]{1,0:T(8,128)}) fusion(bf16[256,2048]{1,0:T(8,128)(2,1)} %bitcast.42, bf16[1,2048,2048]{2,1,0:T(8,128)(2,1)} %param.25, bf16[256,2048]{1,0:T(8,128)(2,1)} %bitcast.52), kind=kOutput, calls=%fused_computation.15 | convolution fusion | flops 2149580544 | bytes 12583936 | tf_op jit(solution)/shard_map/dot_general | solution.py:37
  15.1 2.9 fusion.7
  18.1 55.2 %all-reduce.3.cloned.1.call-done = bf16[256,2048]{1,0:T(8,128)(2,1)} async-done(((bf16[256,2048]{1,0:T(8,128)(2,1)}), bf16[256,2048]{1,0:T(8,128)(2,1)}) %all-reduce.3.cloned.1.call-update) | async-done | bytes 1048592 | tf_op jit(solution)/shard_map/psum | solution.py:16
  73.3 2.0 fusion.23
  75.6 8.0 %all-gather.3 = f32[4,1,256]{2,1,0:T(1,128)S(1)} all-gather(f32[1,1,256]{2,1,0:T(1,128)S(1)} %bitcast.51), channel_id=3, replica_groups=mesh['section'=4,'dp'=8] {'section'}, dimensions={0}, use_global_device_ids=true | all-gather | bytes 5120 | tf_op jit(solution)/shard_map/all_gather | solution.py:20
  83.6 7.1 %all-gather.2 = f32[4,1,256]{2,1,0:T(1,128)S(1)} all-gather(f32[1,1,256]{2,1,0:T(1,128)S(1)} %bitcast.46), channel_id=2, replica_groups=mesh['section'=4,'dp'=8] {'section'}, dimensions={0}, use_global_device_ids=true | all-gather | bytes 5120 | tf_op jit(solution)/shard_map/all_gather | solution.py:20
  90.9 2.1 fusion.18
  93.1 1.1 copy-done.6
  94.3 2.9 fusion.16
  97.2 0.6 copy-done.15
  97.9 64.8 %all-reduce.5.cloned.1.call-done = f32[256,2048]{1,0:T(8,128)} async-done(((f32[256,2048]{1,0:T(8,128)}), f32[256,2048]{1,0:T(8,128)}) %all-reduce.5.cloned.1.call-update) | async-done | bytes 2097168 | tf_op jit(solution)/shard_map/psum | solution.py:119
  162.7 2.1 multiply_reduce_fusion
  164.9 0.6 copy-done.4
  165.6 0.5 multiply_convert_fusion
  166.0 79.9 %while.30 = (s32[]{:T(128)}, bf16[256,2048]{1,0:T(8,128)(2,1)S(1)}, pred[]{:T(512)}, s32[]{:T(128)}) while((s32[]{:T(128)}, bf16[256,2048]{1,0:T(8,128)(2,1)S(1)}, pred[]{:T(512)}, s32[]{:T(128)}) %tuple.77), condition=%wide.region_9.10_spmd, body=%wide.region_8.9_spmd.sunk | while | flops 524290 | bytes 7340126 | solution.py:141
  166.1 1.3 collective-permute-start
  167.4 25.3 %collective-permute-done = bf16[256,2048]{1,0:T(8,128)(2,1)S(1)} collective-permute-done((bf16[256,2048]{1,0:T(8,128)(2,1)S(1)}, bf16[256,2048]{1,0:T(8,128)(2,1)S(1)}, u32[]{:S(2)}, u32[]{:S(2)}) %collective-permute-start) | collective-permute-done | bytes 1048608 | tf_op jit(solution)/shard_map/while/body/eval_jaxpr/ppermute | solution.py:33
  193.0 1.3 collective-permute-start
  194.3 25.2 %collective-permute-done = bf16[256,2048]{1,0:T(8,128)(2,1)S(1)} collective-permute-done((bf16[256,2048]{1,0:T(8,128)(2,1)S(1)}, bf16[256,2048]{1,0:T(8,128)(2,1)S(1)}, u32[]{:S(2)}, u32[]{:S(2)}) %collective-permute-start) | collective-permute-done | bytes 1048608 | tf_op jit(solution)/shard_map/while/body/eval_jaxpr/ppermute | solution.py:33
  219.5 0.3 broadcast_select_fusion.2
  219.8 1.3 collective-permute-start
  221.1 24.6 %collective-permute-done = bf16[256,2048]{1,0:T(8,128)(2,1)S(1)} collective-permute-done((bf16[256,2048]{1,0:T(8,128)(2,1)S(1)}, bf16[256,2048]{1,0:T(8,128)(2,1)S(1)}, u32[]{:S(2)}, u32[]{:S(2)}) %collective-permute-start) | collective-permute-done | bytes 1048608 | tf_op jit(solution)/shard_map/while/body/eval_jaxpr/ppermute | solution.py:33
  245.7 0.3 broadcast_select_fusion.2
  246.0 2.8 fusion.11
  249.0 1.0 copy-done.5
  250.0 8.3 %fusion.24 = f32[2048,2048]{1,0:T(8,128)} fusion(bf16[256,2048]{1,0:T(8,128)(2,1)S(1)} %get-tuple-element.183, bf16[256,2048]{1,0:T(8,128)(2,1)S(1)} %bitcast.43), kind=kOutput, calls=%fused_computation.42 | convolution fusion | flops 2147483648 | bytes 18874368 | tf_op jit(solution)/shard_map/dot_general | solution.py:43
  258.4 0.9 copy-done.7
  259.7 2.4 multiply_subtract_fusion.2
  262.1 37.8 %reduce-scatter.8.cloned.1.call-done = f32[64,2048]{1,0:T(8,128)} async-done(((f32[512,2048]{1,0:T(8,128)}), f32[64,2048]{1,0:T(8,128)}) %reduce-scatter.8.cloned.1.call-update) | async-done | bytes 524304 | tf_op jit(solution)/shard_map/reduce_scatter | solution.py:151
  299.9 2.4 multiply_subtract_fusion.1
  302.2 166.4 %reduce-scatter.4.cloned.1.call-done = f32[256,2048]{1,0:T(8,128)} async-done(((f32[2048,2048]{1,0:T(8,128)}), f32[256,2048]{1,0:T(8,128)}) %reduce-scatter.4.cloned.1.call-update) | async-done | bytes 2097168 | tf_op jit(solution)/shard_map/reduce_scatter | solution.py:143
  468.7 7.6 %multiply_subtract_fusion = (f32[1,256,2048]{2,1,0:T(8,128)}, f32[1,256,2048]{2,1,0:T(8,128)}, f32[1,256,2048]{2,1,0:T(8,128)}) fusion(f32[1,256,2048]{2,1,0:T(8,128)} %param.27, f32[256,2048]{1,0:T(8,128)} %reduce-scatter.4.cloned.1.call-done, f32[1,256,2048]{2,1,0:T(8,128)} %param.29, f32[1,256,2048]{2,1,0:T(8,128)} %param.28), kind=kLoop, calls=%fused_computation.11 | loop fusion | flops 6815744 | bytes 14680064 | tf_op jit(solution)/shard_map/sub | solution.py:67
  (57 shorter events, 1.9 us)
Async XLA Ops:
  7.2 66.1 %copy-start = (bf16[512,2048]{1,0:T(8,128)(2,1)S(1)}, bf16[512,2048]{1,0:T(8,128)(2,1)}, u32[]{:S(2)}) copy-start(bf16[512,2048]{1,0:T(8,128)(2,1)} %param.26) | copy-start | bytes 6291460
  7.2 66.1 %all-reduce.3.cloned.1.call-start = ((), (), s32[]{:S(2)}) async-start(), calls=%async_computation.3 | async-start | bytes 2097152 | tf_op jit(solution)/shard_map/psum | solution.py:16
  7.2 7.8 %copy-start.13 = (f32[2048]{0:T(1024)S(1)}, f32[2048]{0:T(1024)}, u32[]{:S(2)}) copy-start(f32[2048]{0:T(1024)} %param.24) | copy-start | bytes 24580
  15.1 3.0 copy-start.14
  18.0 144.7 %all-reduce.5.cloned.1.call-start = ((), (), s32[]{:S(2)}) async-start(), calls=%async_computation.4 | async-start | bytes 4194304 | tf_op jit(solution)/shard_map/psum | solution.py:119
  93.0 1.2 copy-start.6
  93.1 165.4 %reduce-scatter.6.cloned.1.call-start = ((), (), s32[]{:S(2)}) async-start(), calls=%async_computation.6 | async-start | bytes 4718592 | tf_op jit(solution)/shard_map/reduce_scatter | solution.py:130
  97.1 0.7 copy-start.15
  97.1 65.6 %copy-start.2 = (f32[256,2048]{1,0:T(8,128)S(1)}, f32[256,2048]{1,0:T(8,128)}, u32[]{:S(2)}) copy-start(f32[256,2048]{1,0:T(8,128)} %get-tuple-element.214) | copy-start | bytes 6291460
  97.1 202.7 %reduce-scatter.8.cloned.1.call-start = ((), (), s32[]{:S(2)}) async-start(), calls=%async_computation.7 | async-start | bytes 4718592 | tf_op jit(solution)/shard_map/reduce_scatter | solution.py:151
  162.7 2.2 copy-start.3
  162.7 2.9 copy-start.4
  166.1 26.6 %collective-permute-start = (bf16[256,2048]{1,0:T(8,128)(2,1)S(1)}, bf16[256,2048]{1,0:T(8,128)(2,1)S(1)}, u32[]{:S(2)}, u32[]{:S(2)}) collective-permute-start(bf16[256,2048]{1,0:T(8,128)(2,1)S(1)} %get-tuple-element.304), channel_id=1, source_target_pairs={{8,0},{16,8},{24,16},{9,1},{17,9},{25,17},{10,2},{18,10},{26,18},{... | collective-permute-start | bytes 3145736 | tf_op jit(solution)/shard_map/while/body/eval_jaxpr/ppermute | solution.py:33
  193.0 26.5 %collective-permute-start = (bf16[256,2048]{1,0:T(8,128)(2,1)S(1)}, bf16[256,2048]{1,0:T(8,128)(2,1)S(1)}, u32[]{:S(2)}, u32[]{:S(2)}) collective-permute-start(bf16[256,2048]{1,0:T(8,128)(2,1)S(1)} %get-tuple-element.304), channel_id=1, source_target_pairs={{8,0},{16,8},{24,16},{9,1},{17,9},{25,17},{10,2},{18,10},{26,18},{... | collective-permute-start | bytes 3145736 | tf_op jit(solution)/shard_map/while/body/eval_jaxpr/ppermute | solution.py:33
  219.8 25.9 %collective-permute-start = (bf16[256,2048]{1,0:T(8,128)(2,1)S(1)}, bf16[256,2048]{1,0:T(8,128)(2,1)S(1)}, u32[]{:S(2)}, u32[]{:S(2)}) collective-permute-start(bf16[256,2048]{1,0:T(8,128)(2,1)S(1)} %get-tuple-element.304), channel_id=1, source_target_pairs={{8,0},{16,8},{24,16},{9,1},{17,9},{25,17},{10,2},{18,10},{26,18},{... | collective-permute-start | bytes 3145736 | tf_op jit(solution)/shard_map/while/body/eval_jaxpr/ppermute | solution.py:33
  248.8 1.2 copy-start.5
  248.8 219.9 %reduce-scatter.4.cloned.1.call-start = ((), (), s32[]{:S(2)}) async-start(), calls=%async_computation.5 | async-start | bytes 18874368 | tf_op jit(solution)/shard_map/reduce_scatter | solution.py:143
  258.3 1.0 copy-start.7
  258.3 1.2 copy-start.8
  258.3 1.4 copy-start.9
  258.4 41.5 %copy-start.10 = (f32[64,2048]{1,0:T(8,128)S(1)}, f32[64,2048]{1,0:T(8,128)}, u32[]{:S(2)}) copy-start(f32[64,2048]{1,0:T(8,128)} %param.33) | copy-start | bytes 1572868
  258.4 41.5 %copy-start.11 = (f32[64,2048]{1,0:T(8,128)S(1)}, f32[64,2048]{1,0:T(8,128)}, u32[]{:S(2)}) copy-start(f32[64,2048]{1,0:T(8,128)} %param.35) | copy-start | bytes 1572868
  258.4 41.5 %copy-start.12 = (f32[64,2048]{1,0:T(8,128)S(1)}, f32[64,2048]{1,0:T(8,128)}, u32[]{:S(2)}) copy-start(f32[64,2048]{1,0:T(8,128)} %param.34) | copy-start | bytes 1572868
  468.7 7.6 %copy-start.1 = (bf16[512,2048]{1,0:T(8,128)(2,1)S(1)}, bf16[512,2048]{1,0:T(8,128)(2,1)}, u32[]{:S(2)}) copy-start(bf16[512,2048]{1,0:T(8,128)(2,1)} %param.26) | copy-start | bytes 6291460
Sparse Core Ops, SparseCore 0:
  18.1 55.1 all-reduce.2
  93.2 69.4 all-reduce.4
  165.0 49.8 reduce-scatter.5
  248.9 50.8 reduce-scatter.7
  302.0 166.5 reduce-scatter.3
where the time goes:
time: 483 us
  waiting for transfers between devices  399 us (83%)
  matrix products  26 us (5%)
  other arithmetic  19 us (4%)
  blocking collectives  15.2 us (3%)
  between operations  13.9 us (3%)
  local copies, waits for them, and re-layouts  4.92 us (1%)
    reduce_scatter x1, waiting for transfers between devices, local(): lax.psum_scatter(out_term, 'dp', scatter_dimension=0, tiled=True)  166 us
    ppermute x3, waiting for transfers between devices, from_behind(): return lax.ppermute(block, axis, route)  75.1 us
    psum x1, waiting for transfers between devices, local(): lax.psum(plain_times(logit_cotangent, head_weight), 'section')  64.8 us
    psum x1, waiting for transfers between devices, broadcast(): return lax.psum(kept, axis)  55.2 us
    reduce_scatter x1, waiting for transfers between devices, local(): lax.psum_scatter(embed_term(embed_master.shape[0] * lax.axis_size('dp')),...  37.8 us
    all_gather x2, blocking collectives, combined_all(): gathered = jax.tree.map(lambda a: lax.all_gather(a, axis), part)  15.2 us
    dot_general x3, matrix products, transposed_times(): lax.dot_general(former, latter, (((0,), (0,)), ((), ())), preferred_eleme...  14 us
    sub x3, other arithmetic, adam_update(): master - learning_rate * (first_next / (jnp.sqrt(second_next) + adam_eps)...  12.3 us
  transfers between devices with their start and end apart: 8, of which 7 were waited for; matrix products, arithmetic and copies ran while one was open for 5% of the time, Pallas kernels for 0%

commit v1 on v0

--- a/solution.py
+++ b/solution.py
@@ -116,7 +116,9 @@
     logit_cotangent = jnp.where(target_flat[:, None] == columns, predicted - 1.0, predicted).astype(
         jnp.bfloat16
     )
-    hidden_cotangent = lax.psum(plain_times(logit_cotangent, head_weight), "section")
+    hidden_cotangent = jnp.sum(
+        lax.all_gather(plain_times(logit_cotangent, head_weight), "section"), axis=0
+    )
     top_cotangent = norm_backward(final, final_inverse, hidden_cotangent * final_gain).astype(
         jnp.bfloat16
     )

time: 483 us -> 507 us (1.050)
  waiting for transfers between devices: 399 us -> 417 us
  other arithmetic: 19 us -> 24.8 us
    all_gather x0 -> x1, waiting for transfers between devices: none -> 82.8 us  [local(): lax.all_gather(plain_times(logit_cotangent, head_weight), 'section')]
    psum x1 -> x0, waiting for transfers between devices: 64.8 us -> none  [local(): lax.psum(plain_times(logit_cotangent, head_weight), 'section')]
    reduce_sum x0 -> x1, other arithmetic: none -> 5.84 us  [local(): jnp.sum(lax.all_gather(plain_times(logit_cotangent, head_weight), 'sectio...]
  transfers between devices with their start and end apart: 8 -> 8, of which waited for: 7 -> 7; matrix products, arithmetic and copies ran while one was open for 5% -> 6% of each run, Pallas kernels for 0% -> 0%
where the time goes in v1:
time: 507 us
  waiting for transfers between devices  417 us (82%)
  matrix products  26 us (5%)
  other arithmetic  24.8 us (5%)
  blocking collectives  15.2 us (3%)
  between operations  13.9 us (3%)
  local copies, waits for them, and re-layouts  5.23 us (1%)
    reduce_scatter x1, waiting for transfers between devices, local(): lax.psum_scatter(out_term, 'dp', scatter_dimension=0, tiled=True)  166 us
    all_gather x1, waiting for transfers between devices, local(): lax.all_gather(plain_times(logit_cotangent, head_weight), 'section')  82.8 us
    ppermute x3, waiting for transfers between devices, from_behind(): return lax.ppermute(block, axis, route)  74.8 us
    psum x1, waiting for transfers between devices, broadcast(): return lax.psum(kept, axis)  55.2 us
    reduce_scatter x1, waiting for transfers between devices, local(): lax.psum_scatter(embed_term(embed_master.shape[0] * lax.axis_size('dp')),...  37.8 us
    all_gather x2, blocking collectives, combined_all(): gathered = jax.tree.map(lambda a: lax.all_gather(a, axis), part)  15.2 us
    dot_general x3, matrix products, transposed_times(): lax.dot_general(former, latter, (((0,), (0,)), ((), ())), preferred_eleme...  14 us
    sub x3, other arithmetic, adam_update(): master - learning_rate * (first_next / (jnp.sqrt(second_next) + adam_eps)...  12.3 us
  transfers between devices with their start and end apart: 8, of which 7 were waited for; matrix products, arithmetic and copies ran while one was open for 6% of the time, Pallas kernels for 0%

profile of v1, /device:TPU:0, one launch (start us, length us, event | category | flops | bytes accessed | tf_op | source)
XLA Modules:
  0.0 506.6 jit_solution(6319605300927098642)
XLA Ops:
  7.3 7.8 %multiply_reduce_fusion.1 = (f32[256]{0:T(256)S(1)}, f32[256,2048]{1,0:T(8,128)}) fusion(bf16[256,2048]{1,0:T(8,128)(2,1)} %bitcast.44, bf16[1,2048,2048]{2,1,0:T(8,128)(2,1)} %param.25, bf16[256,2048]{1,0:T(8,128)(2,1)} %bitcast.54), kind=kOutput, calls=%fused_computation.15 | convolution fusion | flops 2149580544 | bytes 12583936 | tf_op jit(solution)/shard_map/dot_general | solution.py:37
  15.1 2.9 fusion.7
  18.1 55.2 %all-reduce.2.cloned.1.call-done = bf16[256,2048]{1,0:T(8,128)(2,1)} async-done(((bf16[256,2048]{1,0:T(8,128)(2,1)}), bf16[256,2048]{1,0:T(8,128)(2,1)}) %all-reduce.2.cloned.1.call-update) | async-done | bytes 1048592 | tf_op jit(solution)/shard_map/psum | solution.py:16
  73.3 2.0 fusion.23
  75.6 8.0 %all-gather.4 = f32[4,1,256]{2,1,0:T(1,128)S(1)} all-gather(f32[1,1,256]{2,1,0:T(1,128)S(1)} %bitcast.53), channel_id=3, replica_groups=mesh['section'=4,'dp'=8] {'section'}, dimensions={0}, use_global_device_ids=true | all-gather | bytes 5120 | tf_op jit(solution)/shard_map/all_gather | solution.py:20
  83.6 7.1 %all-gather.3 = f32[4,1,256]{2,1,0:T(1,128)S(1)} all-gather(f32[1,1,256]{2,1,0:T(1,128)S(1)} %bitcast.48), channel_id=2, replica_groups=mesh['section'=4,'dp'=8] {'section'}, dimensions={0}, use_global_device_ids=true | all-gather | bytes 5120 | tf_op jit(solution)/shard_map/all_gather | solution.py:20
  90.9 2.1 fusion.18
  93.1 1.1 copy-done.6
  94.3 2.9 fusion.16
  97.2 0.6 copy-done.15
  97.9 82.8 %all-gather.7.cloned.1.call-done = f32[1024,2048]{1,0:T(8,128)} async-done(((f32[256,2048]{1,0:T(8,128)}), f32[1024,2048]{1,0:T(8,128)}) %all-gather.7.cloned.1.call-update) | async-done | bytes 8388624 | tf_op jit(solution)/shard_map/all_gather | solution.py:120
  180.7 5.8 %reduce_sum.38 = f32[256,2048]{1,0:T(8,128)} reduce(f32[4,256,2048]{2,1,0:T(8,128)} %bitcast.43, f32[]{:T(128)} %constant.87.clone.1), dimensions={0}, to_apply=%region_6.7 | reduce | flops 1572864 | bytes 10485764 | tf_op jit(solution)/shard_map/reduce_sum | solution.py:119
  186.5 2.1 multiply_reduce_fusion
  188.8 0.9 copy-done.4
  189.7 0.5 multiply_convert_fusion
  190.2 79.6 %while.30 = (s32[]{:T(128)}, bf16[256,2048]{1,0:T(8,128)(2,1)S(1)}, pred[]{:T(512)}, s32[]{:T(128)}) while((s32[]{:T(128)}, bf16[256,2048]{1,0:T(8,128)(2,1)S(1)}, pred[]{:T(512)}, s32[]{:T(128)}) %tuple.77), condition=%wide.region_9.10_spmd, body=%wide.region_8.9_spmd.sunk | while | flops 524290 | bytes 7340126 | solution.py:143
  190.2 1.3 collective-permute-start
  191.5 25.0 %collective-permute-done = bf16[256,2048]{1,0:T(8,128)(2,1)S(1)} collective-permute-done((bf16[256,2048]{1,0:T(8,128)(2,1)S(1)}, bf16[256,2048]{1,0:T(8,128)(2,1)S(1)}, u32[]{:S(2)}, u32[]{:S(2)}) %collective-permute-start) | collective-permute-done | bytes 1048608 | tf_op jit(solution)/shard_map/while/body/eval_jaxpr/ppermute | solution.py:33
  216.8 1.3 collective-permute-start
  218.1 25.2 %collective-permute-done = bf16[256,2048]{1,0:T(8,128)(2,1)S(1)} collective-permute-done((bf16[256,2048]{1,0:T(8,128)(2,1)S(1)}, bf16[256,2048]{1,0:T(8,128)(2,1)S(1)}, u32[]{:S(2)}, u32[]{:S(2)}) %collective-permute-start) | collective-permute-done | bytes 1048608 | tf_op jit(solution)/shard_map/while/body/eval_jaxpr/ppermute | solution.py:33
  243.6 1.3 collective-permute-start
  244.9 24.6 %collective-permute-done = bf16[256,2048]{1,0:T(8,128)(2,1)S(1)} collective-permute-done((bf16[256,2048]{1,0:T(8,128)(2,1)S(1)}, bf16[256,2048]{1,0:T(8,128)(2,1)S(1)}, u32[]{:S(2)}, u32[]{:S(2)}) %collective-permute-start) | collective-permute-done | bytes 1048608 | tf_op jit(solution)/shard_map/while/body/eval_jaxpr/ppermute | solution.py:33
  269.5 0.3 broadcast_select_fusion.2
  269.7 2.8 fusion.11
  272.8 1.0 copy-done.5
  273.8 8.3 %fusion.24 = f32[2048,2048]{1,0:T(8,128)} fusion(bf16[256,2048]{1,0:T(8,128)(2,1)S(1)} %get-tuple-element.183, bf16[256,2048]{1,0:T(8,128)(2,1)S(1)} %bitcast.45), kind=kOutput, calls=%fused_computation.42 | convolution fusion | flops 2147483648 | bytes 18874368 | tf_op jit(solution)/shard_map/dot_general | solution.py:43
  282.2 0.9 copy-done.7
  283.5 2.4 multiply_subtract_fusion.2
  285.8 37.8 %reduce-scatter.8.cloned.1.call-done = f32[64,2048]{1,0:T(8,128)} async-done(((f32[512,2048]{1,0:T(8,128)}), f32[64,2048]{1,0:T(8,128)}) %reduce-scatter.8.cloned.1.call-update) | async-done | bytes 524304 | tf_op jit(solution)/shard_map/reduce_scatter | solution.py:153
  323.6 2.4 multiply_subtract_fusion.1
  326.0 166.5 %reduce-scatter.4.cloned.1.call-done = f32[256,2048]{1,0:T(8,128)} async-done(((f32[2048,2048]{1,0:T(8,128)}), f32[256,2048]{1,0:T(8,128)}) %reduce-scatter.4.cloned.1.call-update) | async-done | bytes 2097168 | tf_op jit(solution)/shard_map/reduce_scatter | solution.py:145
  492.5 7.6 %multiply_subtract_fusion = (f32[1,256,2048]{2,1,0:T(8,128)}, f32[1,256,2048]{2,1,0:T(8,128)}, f32[1,256,2048]{2,1,0:T(8,128)}) fusion(f32[1,256,2048]{2,1,0:T(8,128)} %param.27, f32[256,2048]{1,0:T(8,128)} %reduce-scatter.4.cloned.1.call-done, f32[1,256,2048]{2,1,0:T(8,128)} %param.29, f32[1,256,2048]{2,1,0:T(8,128)} %param.28), kind=kLoop, calls=%fused_computation.11 | loop fusion | flops 6815744 | bytes 14680064 | tf_op jit(solution)/shard_map/sub | solution.py:67
  (58 shorter events, 2.1 us)
Async XLA Ops:
  7.2 66.1 %copy-start = (bf16[512,2048]{1,0:T(8,128)(2,1)S(1)}, bf16[512,2048]{1,0:T(8,128)(2,1)}, u32[]{:S(2)}) copy-start(bf16[512,2048]{1,0:T(8,128)(2,1)} %param.26) | copy-start | bytes 6291460
  7.2 66.1 %all-reduce.2.cloned.1.call-start = ((), (), s32[]{:S(2)}) async-start(), calls=%async_computation.3 | async-start | bytes 2097152 | tf_op jit(solution)/shard_map/psum | solution.py:16
  7.2 7.8 %copy-start.13 = (f32[2048]{0:T(1024)S(1)}, f32[2048]{0:T(1024)}, u32[]{:S(2)}) copy-start(f32[2048]{0:T(1024)} %param.24) | copy-start | bytes 24580
  15.1 3.0 copy-start.14
  18.0 162.7 %all-gather.7.cloned.1.call-start = ((), (), s32[]{:S(2)}) async-start(), calls=%async_computation.7 | async-start | bytes 10485760 | tf_op jit(solution)/shard_map/all_gather | solution.py:120
  93.0 1.2 copy-start.6
  93.1 189.1 %reduce-scatter.6.cloned.1.call-start = ((), (), s32[]{:S(2)}) async-start(), calls=%async_computation.5 | async-start | bytes 4718592 | tf_op jit(solution)/shard_map/reduce_scatter | solution.py:132
  97.1 0.7 copy-start.15
  97.1 226.5 %reduce-scatter.8.cloned.1.call-start = ((), (), s32[]{:S(2)}) async-start(), calls=%async_computation.6 | async-start | bytes 4718592 | tf_op jit(solution)/shard_map/reduce_scatter | solution.py:153
  180.7 5.8 %copy-start.2 = (f32[256,2048]{1,0:T(8,128)S(1)}, f32[256,2048]{1,0:T(8,128)}, u32[]{:S(2)}) copy-start(f32[256,2048]{1,0:T(8,128)} %get-tuple-element.214) | copy-start | bytes 6291460
  186.5 2.2 copy-start.3
  186.5 3.2 copy-start.4
  190.2 26.3 %collective-permute-start = (bf16[256,2048]{1,0:T(8,128)(2,1)S(1)}, bf16[256,2048]{1,0:T(8,128)(2,1)S(1)}, u32[]{:S(2)}, u32[]{:S(2)}) collective-permute-start(bf16[256,2048]{1,0:T(8,128)(2,1)S(1)} %get-tuple-element.304), channel_id=1, source_target_pairs={{8,0},{16,8},{24,16},{9,1},{17,9},{25,17},{10,2},{18,10},{26,18},{... | collective-permute-start | bytes 3145736 | tf_op jit(solution)/shard_map/while/body/eval_jaxpr/ppermute | solution.py:33
  216.8 26.5 %collective-permute-start = (bf16[256,2048]{1,0:T(8,128)(2,1)S(1)}, bf16[256,2048]{1,0:T(8,128)(2,1)S(1)}, u32[]{:S(2)}, u32[]{:S(2)}) collective-permute-start(bf16[256,2048]{1,0:T(8,128)(2,1)S(1)} %get-tuple-element.304), channel_id=1, source_target_pairs={{8,0},{16,8},{24,16},{9,1},{17,9},{25,17},{10,2},{18,10},{26,18},{... | collective-permute-start | bytes 3145736 | tf_op jit(solution)/shard_map/while/body/eval_jaxpr/ppermute | solution.py:33
  243.6 25.9 %collective-permute-start = (bf16[256,2048]{1,0:T(8,128)(2,1)S(1)}, bf16[256,2048]{1,0:T(8,128)(2,1)S(1)}, u32[]{:S(2)}, u32[]{:S(2)}) collective-permute-start(bf16[256,2048]{1,0:T(8,128)(2,1)S(1)} %get-tuple-element.304), channel_id=1, source_target_pairs={{8,0},{16,8},{24,16},{9,1},{17,9},{25,17},{10,2},{18,10},{26,18},{... | collective-permute-start | bytes 3145736 | tf_op jit(solution)/shard_map/while/body/eval_jaxpr/ppermute | solution.py:33
  272.5 1.2 copy-start.5
  272.6 219.9 %reduce-scatter.4.cloned.1.call-start = ((), (), s32[]{:S(2)}) async-start(), calls=%async_computation.4 | async-start | bytes 18874368 | tf_op jit(solution)/shard_map/reduce_scatter | solution.py:145
  282.1 1.0 copy-start.7
  282.1 1.2 copy-start.8
  282.1 1.4 copy-start.9
  282.1 41.5 %copy-start.10 = (f32[64,2048]{1,0:T(8,128)S(1)}, f32[64,2048]{1,0:T(8,128)}, u32[]{:S(2)}) copy-start(f32[64,2048]{1,0:T(8,128)} %param.33) | copy-start | bytes 1572868
  282.1 41.5 %copy-start.11 = (f32[64,2048]{1,0:T(8,128)S(1)}, f32[64,2048]{1,0:T(8,128)}, u32[]{:S(2)}) copy-start(f32[64,2048]{1,0:T(8,128)} %param.35) | copy-start | bytes 1572868
  282.2 41.5 %copy-start.12 = (f32[64,2048]{1,0:T(8,128)S(1)}, f32[64,2048]{1,0:T(8,128)}, u32[]{:S(2)}) copy-start(f32[64,2048]{1,0:T(8,128)} %param.34) | copy-start | bytes 1572868
  492.5 7.6 %copy-start.1 = (bf16[512,2048]{1,0:T(8,128)(2,1)S(1)}, bf16[512,2048]{1,0:T(8,128)(2,1)}, u32[]{:S(2)}) copy-start(bf16[512,2048]{1,0:T(8,128)(2,1)} %param.26) | copy-start | bytes 6291460
Sparse Core Ops, SparseCore 0:
  18.1 55.1 all-reduce.1
  93.2 87.4 all-gather.6
  183.0 49.8 reduce-scatter.5
  272.7 50.8 reduce-scatter.7
  325.8 166.6 reduce-scatter.3
